TPU v7x, 128 devices: a whole 4x4x4 slice. The times are simulated.
128 devices in a mesh: blk: 16 (over y, z), tm: 8 (over x, core).
Axes of the slice: x: 4, y: 4, z: 4, core: 2. Of those that a mesh axis runs over, the one named last changes fastest.
Arguments:
- solution: float32 [512, 128, 1024], P('blk', 'tm'), may hold values from -6 to 6
- residual: float32 [512, 128, 1024], P('blk', 'tm'), may hold values from -12 to 12
- direction: float32 [512, 128, 1024], P('blk', 'tm'), may hold values from -6 to 6
- noise_var: float32 [512, 128, 1024], P('blk', 'tm'), may hold values from 0.5 to 2
- legendre: bfloat16 [512, 512, 512], P('blk', 'tm'), may hold values from -0.25 to 0.25
- temporal: float32 [512, 128, 128], P('tm'), may hold values from -3 to 3.5, as said below
- order_table: int32 [512], replicated, may hold values from 0 to 511, as said below
Outputs:
- solution_new: float32 [512, 128, 1024], P('blk', 'tm')
- residual_new: float32 [512, 128, 1024], P('blk', 'tm')
- direction_new: float32 [512, 128, 1024], P('blk', 'tm')
Inputs may be any that keep to these rules, and one draw needn't show every extreme that they name: `order_table`: each value 0 to 511 appears once. In each aligned block of 32 entries, entry 16 + k equals 511 minus entry k, so each block holds pairs of orders m and 511 - m. `temporal`: each matrix is symmetric and positive definite.
All inputs are finite; a program needn't handle non-finite values.
Results may differ from a plain program's by a relative error of at most 0.0048.
Values may be sent and summed in bfloat16 or wider, within the bound.
A program may use at most 192 MiB of HBM per device.

v0:
```python
import math
import jax
import jax.numpy as jnp
from jax import lax
from jax.sharding import Mesh
from jax.sharding import PartitionSpec as P

BLK = ("blk_0", "blk_1")
TM = ("tm_0", "tm_1")
BLK_TM = ("blk_0", "blk_1", "tm_0", "tm_1")


def trig_table(orders, length):
    points = jnp.arange(128, dtype=jnp.int32)
    step = 2.0 * math.pi / length
    scale = 1.0 / math.sqrt(length / 2.0)
    fine = (orders[:, None] * points[None, :] % length).astype(jnp.float32) * step
    cos_fine, sin_fine = (jnp.cos(fine) * scale, jnp.sin(fine) * scale)
    coarse = jnp.arange(length // 128, dtype=jnp.int32) * 128
    shift = (orders[:, None] * coarse[None, :] % length).astype(jnp.float32) * step
    cos_shift, sin_shift = (jnp.cos(shift), jnp.sin(shift))
    cos_parts, sin_parts = ([], [])
    for q in range(length // 128):
        a, b = (cos_shift[:, q : q + 1], sin_shift[:, q : q + 1])
        cos_parts.append((cos_fine * a - sin_fine * b).astype(jnp.bfloat16))
        sin_parts.append((sin_fine * a + cos_fine * b).astype(jnp.bfloat16))
    return (jnp.concatenate(cos_parts, axis=1), jnp.concatenate(sin_parts, axis=1))


def body(solution, residual, direction, noise_var, legendre, temporal, order_table):
    per_device, deg_dev, lat_all = legendre.shape
    lat_dev, time_dev, longitude = direction.shape
    blocks = lat_all // lat_dev
    cos_table, sin_table = trig_table(order_table, longitude)
    table = jnp.stack(
        [
            cos_table.reshape(blocks, per_device, longitude),
            sin_table.reshape(blocks, per_device, longitude),
        ],
        axis=1,
    )
    own_orders = lax.dynamic_slice_in_dim(order_table, lax.axis_index(BLK) * per_device, per_device)
    own_degrees = lax.axis_index(TM) * deg_dev + jnp.arange(deg_dev, dtype=jnp.int32)
    keep_mask = own_degrees[None, :, None] >= own_orders[:, None, None]
    masked = jnp.where(keep_mask, legendre, jnp.zeros_like(legendre))
    flat = table.reshape(-1, longitude)
    spectra = jnp.einsum(
        "kj,atj->kta", flat, direction.astype(jnp.bfloat16), preferred_element_type=jnp.float32
    ).astype(jnp.bfloat16)
    cycles = lax.all_to_all(
        spectra.reshape(blocks, 2 * per_device * time_dev * lat_dev),
        BLK,
        split_axis=0,
        concat_axis=0,
        tiled=True,
    )
    cycles = cycles.reshape(blocks, 2, per_device, time_dev, lat_dev)
    cycles = cycles.transpose(2, 1, 3, 0, 4).reshape(per_device, 2, time_dev, lat_all)
    cycles = lax.all_gather(cycles, TM, axis=2, tiled=True)
    coeffs = jnp.einsum(
        "icta,ila->lict", cycles, masked, preferred_element_type=jnp.float32
    ).astype(jnp.bfloat16)
    mixed = jnp.einsum(
        "lict,ltu->licu", coeffs, temporal.astype(jnp.bfloat16), preferred_element_type=jnp.float32
    ).astype(jnp.bfloat16)
    terms = jnp.einsum("ila,licu->icua", masked, mixed, preferred_element_type=jnp.float32).astype(
        jnp.bfloat16
    )
    terms = lax.psum_scatter(terms, TM, scatter_dimension=2, tiled=True)
    terms = terms.reshape(per_device, 2, time_dev, blocks, lat_dev).transpose(3, 1, 0, 2, 4)
    entries = lax.all_to_all(
        terms.reshape(blocks, -1), BLK, split_axis=0, concat_axis=0, tiled=True
    )
    entries = entries.reshape(blocks * 2 * per_device, time_dev, lat_dev)
    synthesis = jnp.einsum("kta,kj->atj", entries, flat, preferred_element_type=jnp.float32)
    product = synthesis + noise_var * direction
    sums = jnp.stack(
        [
            jnp.sum(residual * residual),
            jnp.sum(direction * product),
            jnp.sum(residual * product),
            jnp.sum(product * product),
        ]
    )
    norm_now, curvature, cross, square = lax.psum(sums, BLK_TM)
    step_size = norm_now / curvature
    norm_next = norm_now - 2.0 * step_size * cross + step_size * step_size * square
    residual_new = residual - step_size * product
    return (
        solution + step_size * direction,
        residual_new,
        residual_new + norm_next / norm_now * direction,
    )


def solution(mesh):
    torus = Mesh(mesh.devices.reshape(4, 4, 4, 2), ("blk_0", "blk_1", "tm_0", "tm_1"))
    return jax.shard_map(
        body,
        mesh=torus,
        in_specs=(
            P(BLK, TM, None),
            P(BLK, TM, None),
            P(BLK, TM, None),
            P(BLK, TM, None),
            P(BLK, TM, None),
            P(TM, None, None),
            P(),
        ),
        out_specs=(P(BLK, TM, None), P(BLK, TM, None), P(BLK, TM, None)),
        check_vma=False,
    )
```

profile of v0, /device:TPU:1, one launch (start us, length us, event | category | flops | bytes accessed | tf_op | source)
XLA Modules:
  0.0 380.3 jit_solution(8376682952619648902)
XLA Ops:
  10.2 1.8 convert_element_type.275
  24.7 1.5 fusion.13
  26.1 4.8 %copy.39 = bf16[1024,16,32]{2,1,0:T(8,128)(2,1)} copy(bf16[1024,16,32]{0,2,1:T(8,128)(2,1)S(1)} %fusion.13) | data formatting | bytes 2097152 | tf_op jit(solution)/shard_map/convert_element_type | solution.py:49
  30.9 6.3 %all_to_all.16 = bf16[16,1,32768]{2,1,0:T(2,128)(2,1)S(1)} reshape(bf16[1024,16,32]{2,1,0:T(8,128)(2,1)} %copy.39) | data formatting | bytes 2097152 | tf_op jit(solution)/shard_map/all_to_all | solution.py:50
  37.7 7.0 %reduce.66 = bf16[16,32768]{1,0:T(8,128)(2,1)S(1)} reduce(bf16[16,1,32768]{2,1,0:T(2,128)(2,1)S(1)} %all_to_all.16, bf16[]{:T(256)} %broadcast.1093), dimensions={1}, to_apply=%all_to_all.16.reduce_sub_computation | reduce | bytes 2097154 | tf_op jit(solution)/shard_map/all_to_all | solution.py:50
  45.6 24.6 %all_to_all.20 = bf16[16,2,16384]{2,1,0:T(2,128)(2,1)S(1)} all-to-all(bf16[16,2,16384]{2,1,0:T(2,128)(2,1)S(1)} %reshape.811), channel_id=1, replica_groups=mesh['blk_0'=4,'blk_1'=4,'tm_0'=4,'tm_1'=2] {'blk_0','blk_1'}, dimensions={0} | all-to-all | bytes 2097152 | tf_op jit(solution)/shard_map/all_to_all | solution.py:50
  71.2 6.4 %reduce.16 = bf16[16,32768]{1,0:T(8,128)(2,1)S(1)} reduce(bf16[16,1,32768]{2,1,0:T(2,128)(2,1)S(1)} %reshape.812, bf16[]{:T(256)} %constant.78), dimensions={1}, to_apply=%all_to_all.13.reduce_sub_computation | reduce | bytes 2097154 | tf_op jit(solution)/shard_map/all_to_all | solution.py:50
  77.6 5.0 %reshape.718 = bf16[16,2,32,16,32]{4,3,2,1,0:T(8,128)(2,1)} reshape(bf16[16,32768]{1,0:T(8,128)(2,1)S(1)} %reduce.16) | data formatting | bytes 2097152 | tf_op jit(solution)/shard_map/reshape | solution.py:57
  82.6 9.0 %copy.41 = bf16[32,2,16,16,32]{4,3,2,1,0:T(8,128)(2,1)} copy(bf16[32,2,16,16,32]{4,2,0,1,3:T(8,128)(2,1)} %bitcast.51) | data formatting | bytes 2097152 | tf_op jit(solution)/shard_map/transpose | solution.py:58
  91.6 6.9 %reshape.719 = bf16[32,2,16,512]{3,2,1,0:T(8,128)(2,1)} reshape(bf16[32,2,16,16,32]{4,3,2,1,0:T(8,128)(2,1)} %copy.41) | data formatting | bytes 2097152 | tf_op jit(solution)/shard_map/reshape | solution.py:58
  99.5 48.7 %all-gather.2.cloned.1.call-done = bf16[32,2,128,512]{3,2,1,0:T(8,128)(2,1)} async-done(((bf16[32,2,16,512]{3,2,1,0:T(8,128)(2,1)}), bf16[32,2,128,512]{3,2,1,0:T(8,128)(2,1)}) %all-gather.2.cloned.1.call-update) | async-done | bytes 8388624 | tf_op jit(solution)/shard_map/all_gather | solution.py:59
  148.2 6.2 %fusion.14 = bf16[64,32,2,128]{3,0,2,1:T(8,128)(2,1)S(1)} fusion(bf16[32,2,128,512]{3,2,1,0:T(8,128)(2,1)} %all-gather.2.cloned.1.call-done, bf16[32,64,512]{2,1,0:T(8,128)(2,1)S(1)} %copy-done.3, pred[32,64]{1,0:T(8,128)(4,1)S(1)} %broadcast_compare_fusion), kind=kOutput, calls=%fused_computation.23 | convolution fusion | flops 538443776 | bytes 11536384 | tf_op jit(solution)/shard_map/icta,ila->lict/dot_general | solution.py:60
  155.7 4.9 %convolution_convert_fusion = bf16[32,2,128,512]{3,2,1,0:T(8,128)(2,1)} fusion(bf16[32,64,512]{2,1,0:T(8,128)(2,1)S(1)} %copy-done.3, pred[32,64]{1,0:T(8,128)(4,1)S(1)} %broadcast_compare_fusion, bf16[64,32,2,128]{3,1,2,0:T(8,128)(2,1)S(1)} %fusion.10), kind=kOutput, calls=%fused_computation | convolution fusion | flops 542113792 | bytes 11536384 | tf_op jit(solution)/shard_map/ila,licu->icua/dot_general | solution.py:66
  160.6 51.8 %reduce-scatter.2.cloned.1.call-done = bf16[32,2,16,512]{3,2,1,0:T(8,128)(2,1)} async-done(((bf16[32,2,128,512]{3,2,1,0:T(8,128)(2,1)}), bf16[32,2,16,512]{3,2,1,0:T(8,128)(2,1)}) %reduce-scatter.2.cloned.1.call-update) | async-done | bytes 1048592 | tf_op jit(solution)/shard_map/reduce_scatter | solution.py:69
  212.4 5.9 %reshape.720 = bf16[32,2,16,16,32]{4,3,2,1,0:T(8,128)(2,1)} reshape(bf16[32,2,16,512]{3,2,1,0:T(8,128)(2,1)} %reduce-scatter.2.cloned.1.call-done) | data formatting | bytes 2097152 | tf_op jit(solution)/shard_map/reshape | solution.py:70
  218.3 5.2 %copy.80 = bf16[32,2,16,16,32]{4,2,0,1,3:T(8,128)(2,1)} copy(bf16[32,2,16,16,32]{4,3,2,1,0:T(8,128)(2,1)} %reshape.720) | data formatting | bytes 2097152 | tf_op jit(solution)/shard_map/reshape | solution.py:70
  223.6 6.1 %all_to_all.17 = bf16[16,1,32768]{2,1,0:T(2,128)(2,1)S(1)} reshape(bf16[16,2,32,16,32]{4,3,2,1,0:T(8,128)(2,1)} %bitcast.52) | data formatting | bytes 2097152 | tf_op jit(solution)/shard_map/all_to_all | solution.py:71
  229.6 7.0 %reduce.67 = bf16[16,32768]{1,0:T(8,128)(2,1)S(1)} reduce(bf16[16,1,32768]{2,1,0:T(2,128)(2,1)S(1)} %all_to_all.17, bf16[]{:T(256)} %broadcast.1093), dimensions={1}, to_apply=%all_to_all.17.reduce_sub_computation | reduce | bytes 2097154 | tf_op jit(solution)/shard_map/all_to_all | solution.py:71
  236.7 1.6 reshape.813
  238.2 6.9 %all-to-all-start.1 = ((bf16[16,2,16384]{2,1,0:T(2,128)(2,1)}), bf16[16,2,16384]{2,1,0:T(2,128)(2,1)S(1)}, u32[]{:S(2)}, u32[]{:S(2)}) async-start(bf16[16,2,16384]{2,1,0:T(2,128)(2,1)} %reshape.813), calls=%async_computation.2 | async-start | bytes 2097152 | tf_op jit(solution)/shard_map/all_to_all | solution.py:71
  246.3 14.2 %all-to-all-done.1 = bf16[16,2,16384]{2,1,0:T(2,128)(2,1)S(1)} async-done(((bf16[16,2,16384]{2,1,0:T(2,128)(2,1)}), bf16[16,2,16384]{2,1,0:T(2,128)(2,1)S(1)}, u32[]{:S(2)}, u32[]{:S(2)}) %all-to-all-start.1) | async-done | bytes 1048608 | tf_op jit(solution)/shard_map/all_to_all | solution.py:71
  261.6 6.4 %reduce.17 = bf16[16,32768]{1,0:T(8,128)(2,1)S(1)} reduce(bf16[16,1,32768]{2,1,0:T(2,128)(2,1)S(1)} %reshape.814, bf16[]{:T(256)} %constant.78), dimensions={1}, to_apply=%all_to_all.15.reduce_sub_computation | reduce | bytes 2097154 | tf_op jit(solution)/shard_map/all_to_all | solution.py:71
  267.9 4.6 %reshape.721 = bf16[1024,16,32]{2,1,0:T(8,128)(2,1)} reshape(bf16[16,32768]{1,0:T(8,128)(2,1)S(1)} %reduce.17) | data formatting | bytes 2097152 | tf_op jit(solution)/shard_map/reshape | solution.py:74
  272.5 4.7 %copy.46 = bf16[1024,16,32]{0,2,1:T(8,128)(2,1)S(1)} copy(bf16[1024,16,32]{2,1,0:T(8,128)(2,1)} %reshape.721) | data formatting | bytes 2097152 | tf_op jit(solution)/shard_map/reshape | solution.py:74
  277.2 3.0 fusion.71
  280.7 5.6 %multiply_reduce_fusion.2 = (f32[]{:T(128)}, f32[]{:T(128)}, f32[]{:T(128)}, f32[32,16,1024]{2,0,1:T(8,128)}) fusion(f32[32,16,1024]{2,1,0:T(8,128)S(1)} %copy-done, f32[32,16,1024]{2,1,0:T(8,128)S(1)} %copy-done.2, f32[32,16,1024]{2,0,1:T(8,128)S(1)} %bitcast.55, f32[32,16,1024]{2,1,0:T(8,128)S(1)} %copy-done.6), kind=kLoop, calls=%fused_computation.15 | loop fusion | flops 4194301 | bytes 10485772 | tf_op jit(solution)/shard_map/reduce_sum | solution.py:80
  286.3 2.7 pad_maximum_fusion.1
  289.0 65.2 %psum.7 = f32[4]{0:T(128)S(1)} all-reduce(f32[4]{0:T(128)S(1)} %pad_maximum_fusion.1), channel_id=1, replica_groups=mesh['blk_0'=4,'blk_1'=4,'tm_0'=4,'tm_1'=2] {'blk_0','blk_1','tm_0','tm_1'}, use_global_device_ids=true, to_apply=%region_5.6 | all-reduce | flops 4 | bytes 32 | tf_op jit(solution)/shard_map/psum | solution.py:85
  358.6 6.8 %multiply_add_fusion = (f32[32,16,1024]{2,0,1:T(8,128)S(1)}, f32[32,16,1024]{2,0,1:T(8,128)S(1)}, f32[32,16,1024]{2,0,1:T(8,128)S(1)}) fusion(f32[32,16,1024]{2,1,0:T(8,128)S(1)} %copy-done, f32[]{:T(128)S(6)} %div.7, f32[32,16,1024]{2,0,1:T(8,128)} %get-tuple-element.33, f32[]{:T(128)S(6)} %div.6, f32[32,16,1024]{2,1,0:T(8,128)} %param.8, ...), kind=kLoop, calls=%fused_computation.11 | loop fusion | flops 3145728 | bytes 14680072 | tf_op jit(solution)/shard_map/add | solution.py:92
  365.4 2.5 copy.55
  367.9 2.5 copy.56
  370.5 2.5 copy.57
  (57 shorter events, 23.5 us)
Async XLA Ops:
  7.2 141.0 %all-gather.2.cloned.1.call-start = ((), (), s32[]{:S(2)}) async-start(), calls=%async_computation.3 | async-start | bytes 9437184 | tf_op jit(solution)/shard_map/all_gather | solution.py:59
  23.4 1.3 copy-start.5
  91.6 56.6 %copy-start.3 = (bf16[32,64,512]{2,1,0:T(8,128)(2,1)S(1)}, bf16[32,64,512]{2,1,0:T(8,128)(2,1)}, u32[]{:S(2)}) copy-start(bf16[32,64,512]{2,1,0:T(8,128)(2,1)} %param.11) | copy-start | bytes 6291460
  98.6 113.8 %reduce-scatter.2.cloned.1.call-start = ((), (), s32[]{:S(2)}) async-start(), calls=%async_computation.4 | async-start | bytes 9437184 | tf_op jit(solution)/shard_map/reduce_scatter | solution.py:69
  148.2 6.2 %copy-start.4 = (f32[64,128,128]{2,1,0:T(8,128)S(1)}, f32[64,128,128]{2,1,0:T(8,128)}, u32[]{:S(2)}) copy-start(f32[64,128,128]{2,1,0:T(8,128)} %param.12) | copy-start | bytes 12582916
  236.6 8.5 %copy-start.1 = (f32[32,16,1024]{2,1,0:T(8,128)S(1)}, f32[32,16,1024]{2,1,0:T(8,128)}, u32[]{:S(2)}) copy-start(f32[32,16,1024]{2,1,0:T(8,128)} %param.8) | copy-start | bytes 6291460
  238.2 22.3 %all-to-all-start.1 = ((bf16[16,2,16384]{2,1,0:T(2,128)(2,1)}), bf16[16,2,16384]{2,1,0:T(2,128)(2,1)S(1)}, u32[]{:S(2)}, u32[]{:S(2)}) async-start(bf16[16,2,16384]{2,1,0:T(2,128)(2,1)} %reshape.813), calls=%async_computation.2 | async-start | bytes 2097152 | tf_op jit(solution)/shard_map/all_to_all | solution.py:71
  277.2 3.0 copy-start
  277.2 3.0 copy-start.2
  277.2 3.5 copy-start.6
Sparse Core Ops, SparseCore 0:
  98.7 49.4 all-gather.1
  160.7 51.6 reduce-scatter.1
where the time goes:
time: 387 us; the launch traced here: 380 us
  waiting for transfers between devices  115 us (30%)
  blocking collectives  89.8 us (23%)
  local copies, waits for them, and re-layouts  76.3 us (20%)
  other arithmetic  57.2 us (15%)
  between operations  18.5 us (5%)
  matrix products  16.8 us (4%)
  starting transfers between devices  7 us (2%)
    psum x1, blocking collectives, body(): norm_now, curvature, cross, square = lax.psum(sums, BLK_TM)  65.2 us
    reduce_scatter x1, waiting for transfers between devices, body(): terms = lax.psum_scatter(terms, TM, scatter_dimension=2, tiled=True)  51.8 us
    all_gather x1, waiting for transfers between devices, body(): cycles = lax.all_gather(cycles, TM, axis=2, tiled=True)  48.7 us
    all_to_all x1, blocking collectives, body(): lax.all_to_all(spectra.reshape(blocks, 2 * per_device * time_dev * lat_de...  24.6 us
    all_to_all x1, waiting for transfers between devices, body(): lax.all_to_all(terms.reshape(blocks, -1), BLK, split_axis=0, concat_axis=...  14.2 us
    unnamed x21, local copies, waits for them, and re-layouts  13.9 us
    all_to_all x2, other arithmetic, body(): lax.all_to_all(terms.reshape(blocks, -1), BLK, split_axis=0, concat_axis=...  13.4 us
    all_to_all x2, other arithmetic, body(): lax.all_to_all(spectra.reshape(blocks, 2 * per_device * time_dev * lat_de...  13.4 us
  transfers between devices with their start and end apart: 3, of which 3 were waited for; matrix products, arithmetic and copies ran while one was open for 1% of the time, Pallas kernels for 0%

commit v1 on v0

--- a/solution.py
+++ b/solution.py
@@ -82,7 +82,7 @@
             jnp.sum(product * product),
         ]
     )
-    norm_now, curvature, cross, square = lax.psum(sums, BLK_TM)
+    norm_now, curvature, cross, square = jnp.sum(lax.all_gather(sums, BLK_TM), axis=0)
     step_size = norm_now / curvature
     norm_next = norm_now - 2.0 * step_size * cross + step_size * step_size * square
     residual_new = residual - step_size * product

time: 387 us -> 388 us (level)
    unnamed x0 -> x1, blocking collectives: none -> 65.4 us
    psum x1 -> x0, blocking collectives: 65.2 us -> none  [body(): norm_now, curvature, cross, square = lax.psum(sums, BLK_TM)]
    unnamed x7 -> x8, other arithmetic: 9.75 us -> 12.5 us
    unnamed x21 -> x22, local copies, waits for them, and re-layouts: 13.9 us -> 13.9 us
where the time goes in v1:
time: 388 us; the launch traced here: 381 us
  waiting for transfers between devices  115 us (30%)
  blocking collectives  90 us (23%)
  local copies, waits for them, and re-layouts  76.2 us (20%)
  other arithmetic  57.3 us (15%)
  between operations  18.5 us (5%)
  matrix products  16.8 us (4%)
  starting transfers between devices  7 us (2%)
    unnamed x1, blocking collectives  65.4 us
    reduce_scatter x1, waiting for transfers between devices, body(): terms = lax.psum_scatter(terms, TM, scatter_dimension=2, tiled=True)  51.8 us
    all_gather x1, waiting for transfers between devices, body(): cycles = lax.all_gather(cycles, TM, axis=2, tiled=True)  48.7 us
    all_to_all x1, blocking collectives, body(): lax.all_to_all(spectra.reshape(blocks, 2 * per_device * time_dev * lat_de...  24.6 us
    all_to_all x1, waiting for transfers between devices, body(): lax.all_to_all(terms.reshape(blocks, -1), BLK, split_axis=0, concat_axis=...  14.2 us
    unnamed x22, local copies, waits for them, and re-layouts  13.9 us
    all_to_all x2, other arithmetic, body(): lax.all_to_all(terms.reshape(blocks, -1), BLK, split_axis=0, concat_axis=...  13.4 us
    all_to_all x2, other arithmetic, body(): lax.all_to_all(spectra.reshape(blocks, 2 * per_device * time_dev * lat_de...  13.4 us
  transfers between devices with their start and end apart: 3, of which 3 were waited for; matrix products, arithmetic and copies ran while one was open for 1% of the time, Pallas kernels for 0%

profile of v1, /device:TPU:1, one launch (start us, length us, event | category | flops | bytes accessed | tf_op | source)
XLA Modules:
  0.0 380.5 jit_solution(508148013894742451)
XLA Ops:
  10.2 1.8 convert_element_type.275
  24.7 1.5 fusion.13
  26.1 4.8 %copy.39 = bf16[1024,16,32]{2,1,0:T(8,128)(2,1)} copy(bf16[1024,16,32]{0,2,1:T(8,128)(2,1)S(1)} %fusion.13) | data formatting | bytes 2097152 | tf_op jit(solution)/shard_map/convert_element_type | solution.py:49
  30.9 6.3 %all_to_all.16 = bf16[16,1,32768]{2,1,0:T(2,128)(2,1)S(1)} reshape(bf16[1024,16,32]{2,1,0:T(8,128)(2,1)} %copy.39) | data formatting | bytes 2097152 | tf_op jit(solution)/shard_map/all_to_all | solution.py:50
  37.7 7.0 %reduce.66 = bf16[16,32768]{1,0:T(8,128)(2,1)S(1)} reduce(bf16[16,1,32768]{2,1,0:T(2,128)(2,1)S(1)} %all_to_all.16, bf16[]{:T(256)} %broadcast.1094), dimensions={1}, to_apply=%all_to_all.16.reduce_sub_computation | reduce | bytes 2097154 | tf_op jit(solution)/shard_map/all_to_all | solution.py:50
  45.6 24.6 %all_to_all.20 = bf16[16,2,16384]{2,1,0:T(2,128)(2,1)S(1)} all-to-all(bf16[16,2,16384]{2,1,0:T(2,128)(2,1)S(1)} %reshape.814), channel_id=1, replica_groups=mesh['blk_0'=4,'blk_1'=4,'tm_0'=4,'tm_1'=2] {'blk_0','blk_1'}, dimensions={0} | all-to-all | bytes 2097152 | tf_op jit(solution)/shard_map/all_to_all | solution.py:50
  71.2 6.4 %reduce.16 = bf16[16,32768]{1,0:T(8,128)(2,1)S(1)} reduce(bf16[16,1,32768]{2,1,0:T(2,128)(2,1)S(1)} %reshape.815, bf16[]{:T(256)} %constant.82), dimensions={1}, to_apply=%all_to_all.13.reduce_sub_computation | reduce | bytes 2097154 | tf_op jit(solution)/shard_map/all_to_all | solution.py:50
  77.6 5.0 %reshape.718 = bf16[16,2,32,16,32]{4,3,2,1,0:T(8,128)(2,1)} reshape(bf16[16,32768]{1,0:T(8,128)(2,1)S(1)} %reduce.16) | data formatting | bytes 2097152 | tf_op jit(solution)/shard_map/reshape | solution.py:57
  82.6 9.0 %copy.41 = bf16[32,2,16,16,32]{4,3,2,1,0:T(8,128)(2,1)} copy(bf16[32,2,16,16,32]{4,2,0,1,3:T(8,128)(2,1)} %bitcast.51) | data formatting | bytes 2097152 | tf_op jit(solution)/shard_map/transpose | solution.py:58
  91.6 6.9 %reshape.719 = bf16[32,2,16,512]{3,2,1,0:T(8,128)(2,1)} reshape(bf16[32,2,16,16,32]{4,3,2,1,0:T(8,128)(2,1)} %copy.41) | data formatting | bytes 2097152 | tf_op jit(solution)/shard_map/reshape | solution.py:58
  99.5 48.7 %all-gather.3.cloned.1.call-done = bf16[32,2,128,512]{3,2,1,0:T(8,128)(2,1)} async-done(((bf16[32,2,16,512]{3,2,1,0:T(8,128)(2,1)}), bf16[32,2,128,512]{3,2,1,0:T(8,128)(2,1)}) %all-gather.3.cloned.1.call-update) | async-done | bytes 8388624 | tf_op jit(solution)/shard_map/all_gather | solution.py:59
  148.2 6.2 %fusion.14 = bf16[64,32,2,128]{3,0,2,1:T(8,128)(2,1)S(1)} fusion(bf16[32,2,128,512]{3,2,1,0:T(8,128)(2,1)} %all-gather.3.cloned.1.call-done, bf16[32,64,512]{2,1,0:T(8,128)(2,1)S(1)} %copy-done.3, pred[32,64]{1,0:T(8,128)(4,1)S(1)} %broadcast_compare_fusion), kind=kOutput, calls=%fused_computation.23 | convolution fusion | flops 538443776 | bytes 11536384 | tf_op jit(solution)/shard_map/icta,ila->lict/dot_general | solution.py:60
  155.7 4.9 %convolution_convert_fusion = bf16[32,2,128,512]{3,2,1,0:T(8,128)(2,1)} fusion(bf16[32,64,512]{2,1,0:T(8,128)(2,1)S(1)} %copy-done.3, pred[32,64]{1,0:T(8,128)(4,1)S(1)} %broadcast_compare_fusion, bf16[64,32,2,128]{3,1,2,0:T(8,128)(2,1)S(1)} %fusion.10), kind=kOutput, calls=%fused_computation | convolution fusion | flops 542113792 | bytes 11536384 | tf_op jit(solution)/shard_map/ila,licu->icua/dot_general | solution.py:66
  160.6 51.8 %reduce-scatter.2.cloned.1.call-done = bf16[32,2,16,512]{3,2,1,0:T(8,128)(2,1)} async-done(((bf16[32,2,128,512]{3,2,1,0:T(8,128)(2,1)}), bf16[32,2,16,512]{3,2,1,0:T(8,128)(2,1)}) %reduce-scatter.2.cloned.1.call-update) | async-done | bytes 1048592 | tf_op jit(solution)/shard_map/reduce_scatter | solution.py:69
  212.4 5.9 %reshape.720 = bf16[32,2,16,16,32]{4,3,2,1,0:T(8,128)(2,1)} reshape(bf16[32,2,16,512]{3,2,1,0:T(8,128)(2,1)} %reduce-scatter.2.cloned.1.call-done) | data formatting | bytes 2097152 | tf_op jit(solution)/shard_map/reshape | solution.py:70
  218.3 5.2 %copy.80 = bf16[32,2,16,16,32]{4,2,0,1,3:T(8,128)(2,1)} copy(bf16[32,2,16,16,32]{4,3,2,1,0:T(8,128)(2,1)} %reshape.720) | data formatting | bytes 2097152 | tf_op jit(solution)/shard_map/reshape | solution.py:70
  223.6 6.1 %all_to_all.17 = bf16[16,1,32768]{2,1,0:T(2,128)(2,1)S(1)} reshape(bf16[16,2,32,16,32]{4,3,2,1,0:T(8,128)(2,1)} %bitcast.52) | data formatting | bytes 2097152 | tf_op jit(solution)/shard_map/all_to_all | solution.py:71
  229.6 7.0 %reduce.67 = bf16[16,32768]{1,0:T(8,128)(2,1)S(1)} reduce(bf16[16,1,32768]{2,1,0:T(2,128)(2,1)S(1)} %all_to_all.17, bf16[]{:T(256)} %broadcast.1094), dimensions={1}, to_apply=%all_to_all.17.reduce_sub_computation | reduce | bytes 2097154 | tf_op jit(solution)/shard_map/all_to_all | solution.py:71
  236.7 1.6 reshape.816
  238.2 6.9 %all-to-all-start.1 = ((bf16[16,2,16384]{2,1,0:T(2,128)(2,1)}), bf16[16,2,16384]{2,1,0:T(2,128)(2,1)S(1)}, u32[]{:S(2)}, u32[]{:S(2)}) async-start(bf16[16,2,16384]{2,1,0:T(2,128)(2,1)} %reshape.816), calls=%async_computation.2 | async-start | bytes 2097152 | tf_op jit(solution)/shard_map/all_to_all | solution.py:71
  246.3 14.2 %all-to-all-done.1 = bf16[16,2,16384]{2,1,0:T(2,128)(2,1)S(1)} async-done(((bf16[16,2,16384]{2,1,0:T(2,128)(2,1)}), bf16[16,2,16384]{2,1,0:T(2,128)(2,1)S(1)}, u32[]{:S(2)}, u32[]{:S(2)}) %all-to-all-start.1) | async-done | bytes 1048608 | tf_op jit(solution)/shard_map/all_to_all | solution.py:71
  261.6 6.4 %reduce.17 = bf16[16,32768]{1,0:T(8,128)(2,1)S(1)} reduce(bf16[16,1,32768]{2,1,0:T(2,128)(2,1)S(1)} %reshape.817, bf16[]{:T(256)} %constant.82), dimensions={1}, to_apply=%all_to_all.15.reduce_sub_computation | reduce | bytes 2097154 | tf_op jit(solution)/shard_map/all_to_all | solution.py:71
  267.9 4.6 %reshape.721 = bf16[1024,16,32]{2,1,0:T(8,128)(2,1)} reshape(bf16[16,32768]{1,0:T(8,128)(2,1)S(1)} %reduce.17) | data formatting | bytes 2097152 | tf_op jit(solution)/shard_map/reshape | solution.py:74
  272.5 4.4 %copy.46 = bf16[1024,16,32]{0,2,1:T(8,128)(2,1)S(1)} copy(bf16[1024,16,32]{2,1,0:T(8,128)(2,1)} %reshape.721) | data formatting | bytes 2097152 | tf_op jit(solution)/shard_map/reshape | solution.py:74
  277.0 3.0 fusion.71
  280.5 5.6 %multiply_reduce_fusion.2 = (f32[]{:T(128)}, f32[]{:T(128)}, f32[]{:T(128)}, f32[32,16,1024]{2,0,1:T(8,128)}) fusion(f32[32,16,1024]{2,1,0:T(8,128)S(1)} %copy-done, f32[32,16,1024]{2,1,0:T(8,128)S(1)} %copy-done.2, f32[32,16,1024]{2,0,1:T(8,128)S(1)} %bitcast.55, f32[32,16,1024]{2,1,0:T(8,128)S(1)} %copy-done.6), kind=kLoop, calls=%fused_computation.15 | loop fusion | flops 4194301 | bytes 10485772 | tf_op jit(solution)/shard_map/reduce_sum | solution.py:80
  286.1 2.8 maximum_dynamic-update-slice_fusion
  288.9 65.4 %all-reduce = f32[512]{0:T(512)S(1)} all-reduce(f32[512]{0:T(512)S(1)} %maximum_dynamic-update-slice_fusion), channel_id=2, replica_groups=mesh['blk_0'=4,'blk_1'=4,'tm_0'=4,'tm_1'=2] {'blk_0','blk_1','tm_0','tm_1'}, use_global_device_ids=true, to_apply=%add | all-reduce | flops 512 | bytes 4096
  358.9 6.8 %multiply_add_fusion = (f32[32,16,1024]{2,0,1:T(8,128)S(1)}, f32[32,16,1024]{2,0,1:T(8,128)S(1)}, f32[32,16,1024]{2,0,1:T(8,128)S(1)}) fusion(f32[32,16,1024]{2,1,0:T(8,128)S(1)} %copy-done, f32[]{:T(128)S(6)} %div.7, f32[32,16,1024]{2,0,1:T(8,128)} %get-tuple-element.33, f32[]{:T(128)S(6)} %div.6, f32[32,16,1024]{2,1,0:T(8,128)} %param.8, ...), kind=kLoop, calls=%fused_computation.11 | loop fusion | flops 3145728 | bytes 14680072 | tf_op jit(solution)/shard_map/add | solution.py:92
  365.7 2.5 copy.55
  368.2 2.5 copy.56
  370.7 2.5 copy.57
  (60 shorter events, 23.6 us)
Async XLA Ops:
  7.2 141.0 %all-gather.3.cloned.1.call-start = ((), (), s32[]{:S(2)}) async-start(), calls=%async_computation.3 | async-start | bytes 9437184 | tf_op jit(solution)/shard_map/all_gather | solution.py:59
  23.4 1.3 copy-start.5
  91.6 56.6 %copy-start.3 = (bf16[32,64,512]{2,1,0:T(8,128)(2,1)S(1)}, bf16[32,64,512]{2,1,0:T(8,128)(2,1)}, u32[]{:S(2)}) copy-start(bf16[32,64,512]{2,1,0:T(8,128)(2,1)} %param.11) | copy-start | bytes 6291460
  98.6 113.8 %reduce-scatter.2.cloned.1.call-start = ((), (), s32[]{:S(2)}) async-start(), calls=%async_computation.4 | async-start | bytes 9437184 | tf_op jit(solution)/shard_map/reduce_scatter | solution.py:69
  148.2 6.2 %copy-start.4 = (f32[64,128,128]{2,1,0:T(8,128)S(1)}, f32[64,128,128]{2,1,0:T(8,128)}, u32[]{:S(2)}) copy-start(f32[64,128,128]{2,1,0:T(8,128)} %param.12) | copy-start | bytes 12582916
  236.6 8.5 %copy-start.1 = (f32[32,16,1024]{2,1,0:T(8,128)S(1)}, f32[32,16,1024]{2,1,0:T(8,128)}, u32[]{:S(2)}) copy-start(f32[32,16,1024]{2,1,0:T(8,128)} %param.8) | copy-start | bytes 6291460
  238.2 22.3 %all-to-all-start.1 = ((bf16[16,2,16384]{2,1,0:T(2,128)(2,1)}), bf16[16,2,16384]{2,1,0:T(2,128)(2,1)S(1)}, u32[]{:S(2)}, u32[]{:S(2)}) async-start(bf16[16,2,16384]{2,1,0:T(2,128)(2,1)} %reshape.816), calls=%async_computation.2 | async-start | bytes 2097152 | tf_op jit(solution)/shard_map/all_to_all | solution.py:71
  277.0 3.0 copy-start
  277.0 3.0 copy-start.2
  277.0 3.5 copy-start.6
Sparse Core Ops, SparseCore 0:
  98.7 49.4 all-gather.2
  160.7 51.6 reduce-scatter.1
